TPU v7x, 32 devices: a 4x4x1 block of a 4x4x8 slice. The times are simulated.
32 devices in a mesh: data: 1 (over z), tp: 32 (over y, x, core).
Axes of the slice: x: 4, y: 4, z: 1, core: 2. Of those that a mesh axis runs over, the one named last changes fastest.
The devices are a block of a 4x4x8 slice.
Arguments:
- x: bfloat16 [8192, 8192], P('data', 'tp')
- w: bfloat16 [8192, 3072], P('tp')
- r: bfloat16 [8192, 3072], P('data')
- g: bfloat16 [3072], replicated
Outputs:
- output: bfloat16 [8192, 3072], P('data')
All inputs are finite; a program needn't handle non-finite values.
Results may differ from a plain program's by a relative error of at most 0.0117065.
Values are sent between devices in bfloat16 or wider.
A program may use at most 768 MiB of HBM per device.

v0:
```python
import jax
import jax.numpy as jnp
from jax import lax
from jax.sharding import PartitionSpec as P

EPS = 1e-6


def solution(mesh):
    tp = mesh.shape["tp"]

    def local(x, w, r, g):
        rows = x.shape[0] // tp
        idx = lax.axis_index("tp")
        p = jnp.dot(x, w, preferred_element_type=jnp.float32).astype(jnp.bfloat16)
        y = lax.psum_scatter(p, "tp", scatter_dimension=0, tiled=True)
        rr = lax.dynamic_slice_in_dim(r, idx * rows, rows, axis=0)
        a = rr.astype(jnp.float32) + y.astype(jnp.float32)
        ms = jnp.mean(a * a, axis=-1, keepdims=True)
        zl = (a * lax.rsqrt(ms + EPS) * g.astype(jnp.float32)).astype(jnp.bfloat16)
        return lax.all_gather(zl, "tp", axis=0, tiled=True)

    return jax.shard_map(
        local,
        mesh=mesh,
        in_specs=(P("data", "tp"), P("tp", None), P("data", None), P(None)),
        out_specs=P("data", None),
        check_vma=False,
    )
```

profile of v0, /device:TPU:97, one launch (start us, length us, event | category | flops | bytes accessed | tf_op | source)
XLA Modules:
  0.0 443.7 jit_solution(1735532645933790017)
XLA Ops:
  6.5 0.0 copy-start
  6.6 0.0 reduce-scatter.2.cloned.1.call-start
  6.6 1.4 copy-done
  8.0 22.8 %convolution_convert_fusion = bf16[8192,3072]{1,0:T(8,128)(2,1)} fusion(bf16[8192,256]{1,0:T(8,128)(2,1)} %param.4, bf16[256,3072]{1,0:T(8,128)(2,1)S(1)} %copy-done), kind=kOutput, calls=%fused_computation | convolution fusion | flops 12910067712 | bytes 56098816 | tf_op jit(solution)/shard_map/dot_general | solution.py:15
  30.7 0.0 copy-start.3
  30.7 0.1 reduce-scatter.2.cloned.1.call-update
  30.8 0.1 all-gather.2.cloned.1.call-start
  30.9 0.6 copy-done.3
  31.4 212.8 %reduce-scatter.2.cloned.1.call-done = bf16[256,3072]{1,0:T(8,128)(2,1)} async-done(((bf16[8192,3072]{1,0:T(8,128)(2,1)}), bf16[256,3072]{1,0:T(8,128)(2,1)}) %reduce-scatter.2.cloned.1.call-update) | async-done | bytes 1572880 | tf_op jit(solution)/shard_map/reduce_scatter | solution.py:16
  244.3 0.0 copy-start.2
  244.3 2.6 multiply_reduce_fusion
  246.9 0.0 copy-done.2
  246.9 3.3 multiply_convert_fusion
  250.1 0.1 all-gather.2.cloned.1.call-update
  250.2 152.6 %all-gather.2.cloned.1.call-done = bf16[8192,3072]{1,0:T(8,128)(2,1)} async-done(((bf16[256,3072]{1,0:T(8,128)(2,1)}), bf16[8192,3072]{1,0:T(8,128)(2,1)}) %all-gather.2.cloned.1.call-update) | async-done | bytes 50331664 | tf_op jit(solution)/shard_map/all_gather | solution.py:21
  402.8 0.0 copy-start.1
  402.8 34.0 %copy.6 = bf16[8192,3072]{1,0:T(8,128)(2,1)} copy(bf16[8192,3072]{1,0:T(8,128)(2,1)} %all-gather.2.cloned.1.call-done) | data formatting | bytes 100663296
  436.9 0.0 copy-done.1
  (2 shorter events, 0.0 us)
Async XLA Ops:
  6.5 1.4 copy-start
  6.6 237.7 %reduce-scatter.2.cloned.1.call-start = ((), (), s32[]{:S(2)}) async-start(), calls=%async_computation.1 | async-start | bytes 51904512 | tf_op jit(solution)/shard_map/reduce_scatter | solution.py:16
  30.7 0.7 copy-start.3
  30.8 372.0 %all-gather.2.cloned.1.call-start = ((), (), s32[]{:S(2)}) async-start(), calls=%async_computation.2 | async-start | bytes 51904512 | tf_op jit(solution)/shard_map/all_gather | solution.py:21
  244.3 2.6 copy-start.2
  402.8 34.0 %copy-start.1 = (bf16[256,3072]{1,0:T(8,128)(2,1)S(1)}, bf16[256,3072]{1,0:T(8,128)(2,1)}, u32[]{:S(2)}) copy-start(bf16[256,3072]{1,0:T(8,128)(2,1)} %param.5) | copy-start | bytes 4718596
Sparse Core Ops, SparseCore 0:
  30.9 213.2 reduce-scatter.1
  250.3 152.4 all-gather.1
where the time goes:
time: 444 us
  waiting for transfers between devices  366 us (82%)
  local copies, waits for them, and re-layouts  36 us (8%)
  matrix products  22.8 us (5%)
  between operations  13.5 us (3%)
  other arithmetic  5.87 us (1%)
    reduce_scatter x1, waiting for transfers between devices, local(): y = lax.psum_scatter(p, 'tp', scatter_dimension=0, tiled=True)  213 us
    all_gather x1, waiting for transfers between devices, local(): return lax.all_gather(zl, 'tp', axis=0, tiled=True)  153 us
    unnamed x9, local copies, waits for them, and re-layouts  36 us
    dot_general x1, matrix products, local(): p = jnp.dot(x, w, preferred_element_type=jnp.float32).astype(jnp.bfloat16)  22.8 us
  transfers between devices with their start and end apart: 2, of which 2 were waited for; matrix products, arithmetic and copies ran while one was open for 0% of the time, Pallas kernels for 0%

commit v1 on v0

v1 whole, which is shorter than its diff:
```python
import functools
import math

import jax
import jax.numpy as jnp
from jax import lax
from jax.experimental import pallas as pl
from jax.experimental.pallas import tpu as pltpu
from jax.sharding import PartitionSpec as P

EPS = 1e-6
CORES = 2
MESH = pl.DeviceIdType.MESH


def _place(side):
    me = lax.axis_index("tp")
    c = lax.rem(me, CORES)
    chip = lax.div(me, CORES)
    xx, yy = lax.rem(chip, side), lax.div(chip, side)
    return me, c, xx + (yy - xx) * c, yy + (xx - yy) * c


def _dev(side, c, i, j):
    return CORES * (i * (1 + (side - 1) * c) + j * (side - (side - 1) * c)) + c


def _send(src, dst, ssem, rsem, dev):
    pltpu.make_async_remote_copy(
        src_ref=src, dst_ref=dst, send_sem=ssem, recv_sem=rsem,
        device_id={"tp": dev}, device_id_type=MESH,
    ).start()


def _wait_recv(ref, sem, dev):
    pltpu.make_async_remote_copy(
        src_ref=ref, dst_ref=ref, send_sem=sem, recv_sem=sem,
        device_id={"tp": dev}, device_id_type=MESH,
    ).wait_recv()


def _wait_send(ref, sem, dev):
    pltpu.make_async_remote_copy(
        src_ref=ref, dst_ref=ref, send_sem=sem, recv_sem=sem,
        device_id={"tp": dev}, device_id_type=MESH,
    ).wait_send()


def _barrier(devs):
    bar = pltpu.get_barrier_semaphore()
    for d in devs:
        pl.semaphore_signal(bar, inc=1, device_id={"tp": d}, device_id_type=MESH)
    pl.semaphore_wait(bar, len(devs))


def _reduce_kernel(
    side, total,
    x_ref, w_ref, r_ref, g_ref, z_ref,
    wg, xl, xg, xr, acc, s2, sp, sm, ra, rb, fm, fp, rt,
    lsem, wrel, wsem, wssem, xrel, xsem, xssem, xrssem, rsem, rssem,
):
    me, c, i, j = _place(side)
    o = 1 - c
    kf = x_ref.shape[1]
    blk = z_ref.shape[0]
    half = blk // 2
    hk = kf // 2
    group = side * blk
    width = wg.shape[1]

    def at(v, d):
        return lax.rem(v + d + side, side)

    ip, im, jp, jm = at(i, 1), at(i, -1), at(j, 1), at(j, -1)
    partner = _dev(side, o, j, i)
    in_p, in_m = _dev(side, c, ip, j), _dev(side, c, im, j)
    red_p, red_m = _dev(side, c, i, jp), _dev(side, c, i, jm)
    ot_p, ot_m = _dev(side, o, jp, i), _dev(side, o, jm, i)
    from_p, from_m = _dev(side, o, j, ip), _dev(side, o, j, im)

    rows0 = c * (total // CORES) + i * group + j * blk
    cw = pltpu.make_async_copy(w_ref, wg.at[pl.ds((i * CORES + c) * kf, kf)], lsem.at[0])
    cw.start()
    cx = pltpu.make_async_copy(x_ref, xl, lsem.at[1])
    cx.start()
    cr = pltpu.make_async_copy(r_ref.at[pl.ds(rows0, blk)], rt, lsem.at[2])
    cr.start()

    _barrier((partner, in_p, in_m, red_p, red_m, ot_p, ot_m, from_p, from_m))
    cw.wait()

    own = (i * CORES + c) * kf
    oth = (j * CORES + c) * kf
    for h in (0, 1):
        src = wg.at[pl.ds(own + h * hk, hk)]
        dst_own = wg.at[pl.ds(own + h * hk, hk)]
        dst_oth = wg.at[pl.ds(oth + h * hk, hk)]
        _send(src, dst_own, wssem, wrel.at[0, c] if h == 0 else wsem, in_p)
        _send(src, dst_oth, wssem, wrel.at[0, c] if h == 0 else wsem, ot_p)
        _send(src, dst_own, wssem, wrel.at[1, c] if h == 1 else wsem, in_m)
        _send(src, dst_oth, wssem, wrel.at[1, c] if h == 1 else wsem, ot_m)
    _send(wg.at[pl.ds(own, kf)], wg.at[pl.ds(oth, kf)], wssem, wsem, partner)

    cx.wait()
    order = (2, 1, -1, 0)

    def send_x(n):
        for cc, a, b, up, down in ((c, i, j, in_p, in_m), (o, j, i, ot_p, ot_m)):
            base = cc * (total // CORES) + at(b, order[n]) * blk
            cols = pl.ds((a * CORES + c) * kf, kf)
            far = base + at(a, 2) * group
            _send(xl.at[pl.ds(far, half)], xr.at[n, 0, c], xssem, xrel.at[n, 0, c], up)
            _send(xl.at[pl.ds(far + half, half)], xr.at[n, 1, c], xssem, xrel.at[n, 1, c], down)
            _send(xl.at[pl.ds(base + at(a, 1) * group, blk)],
                  xg.at[pl.ds(n * blk, blk), cols], xssem, xsem.at[n], up)
            _send(xl.at[pl.ds(base + at(a, -1) * group, blk)],
                  xg.at[pl.ds(n * blk, blk), cols], xssem, xsem.at[n], down)
        base = o * (total // CORES) + j * group + at(i, order[n]) * blk
        _send(xl.at[pl.ds(base, blk)],
              xg.at[pl.ds(n * blk, blk), pl.ds((j * CORES + c) * kf, kf)], xssem, xsem.at[n], partner)
        base = c * (total // CORES) + i * group + at(j, order[n]) * blk
        cols = pl.multiple_of((i * CORES + c) * kf, kf)
        xg[n * blk:(n + 1) * blk, pl.ds(cols, kf)] = xl[pl.ds(pl.multiple_of(base, blk), blk), :]

    def pass_x(n):
        for e in range(CORES):
            _wait_recv(xr.at[n, 0, e], xrel.at[n, 0, e], partner)
            _send(xr.at[n, 0, e], xg.at[pl.ds(n * blk, half), pl.ds((im * CORES + e) * kf, kf)],
                  xrssem, xsem.at[n], in_p)
            _wait_recv(xr.at[n, 1, e], xrel.at[n, 1, e], partner)
            _send(xr.at[n, 1, e], xg.at[pl.ds(n * blk + half, half), pl.ds((ip * CORES + e) * kf, kf)],
                  xrssem, xsem.at[n], in_m)

    for e in range(CORES):
        slot = (im * CORES + e) * kf
        _wait_recv(wg.at[pl.ds(slot, hk)], wrel.at[0, e], partner)
        _send(wg.at[pl.ds(slot, hk)], wg.at[pl.ds(slot, hk)], wssem, wsem, in_p)
        slot = (ip * CORES + e) * kf + hk
        _wait_recv(wg.at[pl.ds(slot, hk)], wrel.at[1, e], partner)
        _send(wg.at[pl.ds(slot, hk)], wg.at[pl.ds(slot, hk)], wssem, wsem, in_m)
    for n in range(side):
        send_x(n)
    pass_x(0)
    _wait_recv(wg.at[pl.ds(0, (2 * side * CORES - 6) * hk)], wsem, partner)

    tile = next(t for t in (512, 256, 128) if width % t == 0)

    def matmul(n):
        _wait_recv(xg.at[pl.ds(n * blk, blk), pl.ds(0, (side * CORES - 1) * kf)], xsem.at[n], partner)

        @pl.loop(0, width // tile)
        def _(t):
            cols = pl.ds(pl.multiple_of(t * tile, tile), tile)
            acc[:, cols] = jnp.dot(
                xg[n * blk:(n + 1) * blk, :], wg[:, cols], preferred_element_type=jnp.float32)

    step = next(s for s in (32, 16, 8) if half % s == 0)

    def rounded(dst, first, add=None):
        @pl.loop(0, half // step)
        def _(t):
            off = pl.multiple_of(t * step, step)
            v = acc[pl.ds(first + off, step), :]
            if add is not None:
                v = v + add[pl.ds(off, step), :].astype(jnp.float32)
            dst[pl.ds(first + off, step), :] = v.astype(dst.dtype)

    lo, hi = pl.ds(0, half), pl.ds(half, half)
    matmul(0)
    rounded(s2, 0)
    _send(s2.at[lo], ra, rssem.at[0], rsem.at[0], red_p)
    rounded(s2, half)
    _send(s2.at[hi], rb, rssem.at[0], rsem.at[1], red_m)
    pass_x(1)
    matmul(1)
    rounded(sp, half)
    _send(sp.at[hi], fm.at[hi], rssem.at[1], rsem.at[2], red_p)
    pass_x(2)
    _wait_recv(ra, rsem.at[0], partner)
    rounded(sp, 0, ra)
    _send(sp.at[lo], fm.at[lo], rssem.at[1], rsem.at[2], red_p)
    matmul(2)
    rounded(sm, 0)
    _send(sm.at[lo], fp.at[lo], rssem.at[2], rsem.at[3], red_m)
    pass_x(3)
    _wait_recv(rb, rsem.at[1], partner)
    rounded(sm, half, rb)
    _send(sm.at[hi], fp.at[hi], rssem.at[2], rsem.at[3], red_m)
    matmul(3)
    cr.wait()
    _wait_recv(fm, rsem.at[2], partner)
    _wait_recv(fp, rsem.at[3], partner)

    @pl.loop(0, blk // step)
    def _(t):
        rows = pl.ds(pl.multiple_of(t * step, step), step)
        y = acc[rows, :] + (fm[rows, :].astype(jnp.float32) + fp[rows, :].astype(jnp.float32))
        a = rt[rows, :].astype(jnp.float32) + y.astype(jnp.bfloat16).astype(jnp.float32)
        ms = jnp.mean(a * a, axis=-1, keepdims=True)
        z_ref[rows, :] = (a * lax.rsqrt(ms + EPS) * g_ref[...].astype(jnp.float32)).astype(z_ref.dtype)

    _wait_send(wg.at[pl.ds(0, 7 * kf)], wssem, partner)
    _wait_send(xg.at[:, pl.ds(0, 7 * kf)], xssem, partner)
    _wait_send(xg.at[:, pl.ds(0, 2 * kf)], xrssem, partner)
    for n, ref in enumerate((s2, sp, sm)):
        _wait_send(ref, rssem.at[n], partner)


def _gather_kernel(side, zl_ref, z_ref, rsem, csem, ssem):
    me, c, i, j = _place(side)
    blk = zl_ref.shape[0]
    q = blk // 4
    base = c * (z_ref.shape[0] // CORES)
    partner = _dev(side, 1 - c, j, i)

    def at(v, d):
        return lax.rem(v + d + side, side)

    near = {
        (0, 1): _dev(side, c, at(i, 1), j), (0, -1): _dev(side, c, at(i, -1), j),
        (1, 1): _dev(side, c, i, at(j, 1)), (1, -1): _dev(side, c, i, at(j, -1)),
    }

    def offset(k, p, s):
        slot = at(i, k[0]) * side + at(j, k[1])
        return base + slot * blk + (2 * p + s) * q, slot * 4 + 2 * p + s

    own = base + (i * side + j) * blk

    @pl.loop(0, blk // 8)
    def _(t):
        row = pl.multiple_of(t * 8, 8)
        z_ref[pl.ds(pl.multiple_of(own + row, 8), 8), :] = zl_ref[pl.ds(row, 8), :]

    _barrier((partner,) + tuple(near.values()))

    def ship(k, p, s, ways):
        off, slot = offset(k, p, s)
        piece = z_ref.at[pl.ds(off, q)]
        for way in ways:
            _send(piece, piece, ssem, rsem.at[slot], near[way])
        _send(piece, piece, ssem, csem, partner)

    def take(k, p, s, ways):
        off, slot = offset(k, p, s)
        _wait_recv(z_ref.at[pl.ds(off, q)], rsem.at[slot], partner)
        ship(k, p, s, ways)

    def vec(p, d, e=0):
        return (d, e) if p == 0 else (e, d)

    both = lambda axis: ((axis, 1), (axis, -1))
    for p in (0, 1):
        for s in (0, 1):
            off, slot = offset((0, 0), p, s)
            piece = z_ref.at[pl.ds(off, q)]
            for way in both(p):
                _send(piece, piece, ssem, rsem.at[slot], near[way])
    for p in (0, 1):
        for s in (0, 1):
            ship((0, 0), p, s, both(1 - p))
    for s in (0, 1):
        for p in (0, 1):
            for d in (-1, 1):
                on = ((p, -d),) if (s == 0) == (d == -1) else ()
                take(vec(p, d), p, s, on + both(1 - p))
    def second(d1):
        for s in (0, 1):
            for p in (0, 1):
                for d in (-1, 1):
                    on = ((1 - p, -d),) if (s == 0) == (d == -1) else ()
                    take(vec(p, d1, d), p, s, on)
    second(0)
    for s in (0, 1):
        for p in (0, 1):
            take(vec(p, 2), p, s, both(1 - p))
    second(-1)
    second(1)
    second(2)
    for d1 in (0, -1, 1, 2):
        for s in (0, 1):
            for p in (0, 1):
                take(vec(p, d1, 2), p, s, ())
    n = side * side * 4
    _wait_recv(z_ref.at[pl.ds(0, n * q)], csem, partner)
    _wait_send(z_ref.at[pl.ds(0, (2 * n - 4) * q)], ssem, partner)


def _store_kernel(z_ref, o_ref, sem):
    copy = pltpu.make_async_copy(z_ref, o_ref, sem)
    copy.start()
    copy.wait()


def solution(mesh):
    tp = mesh.shape["tp"]
    side = math.isqrt(tp // CORES)

    def local(x, w, r, g):
        total, kf = x.shape
        width = w.shape[1]
        blk = total // tp
        bf = jnp.bfloat16
        dma = pltpu.SemaphoreType.DMA
        any_ = pl.BlockSpec(memory_space=pl.ANY)
        vmem = pl.BlockSpec(memory_space=pltpu.VMEM)
        zl = pl.pallas_call(
            functools.partial(_reduce_kernel, side, total),
            out_shape=pltpu.VMEM((blk, width), bf),
            in_specs=[any_, any_, any_, vmem],
            out_specs=vmem,
            scratch_shapes=[
                pltpu.VMEM((side * CORES * kf, width), bf),
                pltpu.VMEM((total, kf), bf),
                pltpu.VMEM((side * blk, side * CORES * kf), bf),
                pltpu.VMEM((side, 2, CORES, blk // 2, kf), bf),
                pltpu.VMEM((blk, width), jnp.float32),
                pltpu.VMEM((blk, width), bf),
                pltpu.VMEM((blk, width), bf),
                pltpu.VMEM((blk, width), bf),
                pltpu.VMEM((blk // 2, width), bf),
                pltpu.VMEM((blk // 2, width), bf),
                pltpu.VMEM((blk, width), bf),
                pltpu.VMEM((blk, width), bf),
                pltpu.VMEM((blk, width), bf),
                dma((3,)), dma((2, CORES)), dma, dma,
                dma((side, 2, CORES)), dma((side,)), dma, dma,
                dma((4,)), dma((3,)),
            ],
            compiler_params=pltpu.CompilerParams(
                collective_id=0, has_side_effects=True, vmem_limit_bytes=56 * 2**20),
            name="reduce",
        )(x, w, r, g.reshape(1, width))
        z = pl.pallas_call(
            functools.partial(_gather_kernel, side),
            out_shape=pltpu.VMEM(r.shape, bf),
            in_specs=[vmem],
            out_specs=vmem,
            scratch_shapes=[dma((side * side * 4,)), dma, dma],
            compiler_params=pltpu.CompilerParams(
                collective_id=1, has_side_effects=True, vmem_limit_bytes=4 * 2**20),
            name="gather",
        )(zl)
        return pl.pallas_call(
            _store_kernel,
            out_shape=pltpu.HBM(r.shape, bf),
            in_specs=[vmem],
            out_specs=pl.BlockSpec(memory_space=pltpu.HBM),
            scratch_shapes=[dma],
            compiler_params=pltpu.CompilerParams(vmem_limit_bytes=2**20),
            name="store",
        )(z)

    return jax.shard_map(
        local,
        mesh=mesh,
        in_specs=(P("data", "tp"), P("tp", None), P("data", None), P(None)),
        out_specs=P("data", None),
        check_vma=False,
    )
```

time: 444 us -> 279 us (0.63)
  waiting for transfers between devices: 366 us -> 0 us
  Pallas kernels: 0 us -> 278 us
  local copies, waits for them, and re-layouts: 36 us -> 1.3 us
  matrix products: 22.8 us -> 0 us
  between operations: 13.5 us -> 0.02 us
  other arithmetic: 5.87 us -> 0 us
    pallas_call x0 -> x3, Pallas kernels: none -> 278 us  [the longest x1 136 us: local(): pl.pallas_call(functools.partial(_gather_kernel, side), out_shape=pltpu.V...]
    reduce_scatter x1 -> x0, waiting for transfers between devices: 213 us -> none  [local(): y = lax.psum_scatter(p, 'tp', scatter_dimension=0, tiled=True)]
    all_gather x1 -> x0, waiting for transfers between devices: 153 us -> none  [local(): return lax.all_gather(zl, 'tp', axis=0, tiled=True)]
    unnamed x9 -> x0, local copies, waits for them, and re-layouts: 36 us -> none
    dot_general x1 -> x0, matrix products: 22.8 us -> none  [local(): p = jnp.dot(x, w, preferred_element_type=jnp.float32).astype(jnp.bfloat16)]
  transfers between devices with their start and end apart: 2 -> 0, of which waited for: 2 -> 0; matrix products, arithmetic and copies ran while one was open for 0% -> 0% of each run, Pallas kernels for 0% -> 0%
where the time goes in v1:
time: 279 us
  Pallas kernels  278 us (100%)
    pallas_call x1, Pallas kernels, local(): pl.pallas_call(functools.partial(_gather_kernel, side), out_shape=pltpu.V...  136 us
    pallas_call x1, Pallas kernels, local(): pl.pallas_call(functools.partial(_reduce_kernel, side, total), out_shape=...  125 us
    pallas_call x1, Pallas kernels, local(): pl.pallas_call(_store_kernel, out_shape=pltpu.HBM(r.shape, bf), in_specs=...  17.2 us

profile of v1, /device:TPU:97, one launch (start us, length us, event | category | flops | bytes accessed | tf_op | source)
XLA Modules:
  0.0 279.0 jit_solution(5795267865524118529)
XLA Ops:
  0.0 1.3 reshape.3.g_ref
  1.3 124.7 %reduce.1.zl_ref = bf16[256,3072]{1,0:T(8,128)(2,1)S(1)} custom-call(bf16[8192,256]{1,0:T(8,128)(2,1)} %x_ref.1, bf16[256,3072]{1,0:T(8,128)(2,1)} %w_ref.1, bf16[8192,3072]{1,0:T(8,128)(2,1)} %r_ref.1, bf16[1,3072]{1,0:T(2,128)(2,1)} %reshape.3.g_ref), custom_call_target="tpu_custom_call" | custom-call | tf_op jit(solution)/shard_map/reduce/pallas_call | solution.py:307
  126.0 135.8 %gather.1.z_ref = bf16[8192,3072]{1,0:T(8,128)(2,1)S(1)} custom-call(bf16[256,3072]{1,0:T(8,128)(2,1)S(1)} %reduce.1.zl_ref), custom_call_target="tpu_custom_call" | custom-call | tf_op jit(solution)/shard_map/gather/pallas_call | solution.py:334
  261.8 17.2 %store.1 = bf16[8192,3072]{1,0:T(8,128)(2,1)} custom-call(bf16[8192,3072]{1,0:T(8,128)(2,1)S(1)} %gather.1.z_ref), custom_call_target="tpu_custom_call" | custom-call | tf_op jit(solution)/shard_map/store/pallas_call | solution.py:344

commit v2 on v0

v2 whole, which is shorter than its diff:
```python
import functools
import math

import jax
import jax.numpy as jnp
from jax import lax
from jax.experimental import pallas as pl
from jax.experimental.pallas import tpu as pltpu
from jax.sharding import PartitionSpec as P

EPS = 1e-6
CORES = 2
MESH = pl.DeviceIdType.MESH


def _place(side):
    me = lax.axis_index("tp")
    c = lax.rem(me, CORES)
    chip = lax.div(me, CORES)
    xx, yy = lax.rem(chip, side), lax.div(chip, side)
    return me, c, xx + (yy - xx) * c, yy + (xx - yy) * c


def _dev(side, c, i, j):
    return CORES * (i * (1 + (side - 1) * c) + j * (side - (side - 1) * c)) + c


def _send(src, dst, ssem, rsem, dev):
    pltpu.make_async_remote_copy(
        src_ref=src, dst_ref=dst, send_sem=ssem, recv_sem=rsem,
        device_id={"tp": dev}, device_id_type=MESH,
    ).start()


def _wait_recv(ref, sem, dev):
    pltpu.make_async_remote_copy(
        src_ref=ref, dst_ref=ref, send_sem=sem, recv_sem=sem,
        device_id={"tp": dev}, device_id_type=MESH,
    ).wait_recv()


def _wait_send(ref, sem, dev):
    pltpu.make_async_remote_copy(
        src_ref=ref, dst_ref=ref, send_sem=sem, recv_sem=sem,
        device_id={"tp": dev}, device_id_type=MESH,
    ).wait_send()


def _barrier(devs):
    bar = pltpu.get_barrier_semaphore()
    for d in devs:
        pl.semaphore_signal(bar, inc=1, device_id={"tp": d}, device_id_type=MESH)
    pl.semaphore_wait(bar, len(devs))


def _fused_kernel(
    side, x_ref, w_ref, r_ref, g_ref, z_ref,
    xg, xr, acc, held,
    lsem, wrel, wsem, wssem, xrel, xsem, xssem, xrssem, rsem, rssem, credit, gsem, csem, gssem,
):
    me, c, i, j = _place(side)
    o = 1 - c
    total, width = z_ref.shape
    kf = x_ref.shape[-1]
    blk = x_ref.shape[3]
    q = blk // side
    hq = q // 2
    hk = kf // 2
    hs = side // 2
    f32 = jnp.float32

    def at(v, d):
        return lax.rem(v + d + side, side)

    ip, im, jp, jm = at(i, 1), at(i, -1), at(j, 1), at(j, -1)
    partner = _dev(side, o, j, i)
    in_p, in_m = _dev(side, c, ip, j), _dev(side, c, im, j)
    red_p, red_m = _dev(side, c, i, jp), _dev(side, c, i, jm)
    ot_p, ot_m = _dev(side, o, jp, i), _dev(side, o, jm, i)
    from_p, from_m = _dev(side, o, j, ip), _dev(side, o, j, im)

    lent, mine = o * (total // CORES), c * (total // CORES)
    own_rows = mine + (i * side + j) * blk
    names = ("s2", "sp", "sm", "fm", "fp", "ra", "rb")
    where = {k: side * CORES * kf + n * blk for n, k in enumerate(names)}

    def wrows(cc, slot, first, size):
        return z_ref.at[pl.ds((1 - cc) * (total // CORES) + slot * kf + first, size)]

    def buf(k, n, first, size):
        return pl.ds(lent + where[k] + n * q + first, size)

    own, oth = i * CORES + c, j * CORES + c
    cw = pltpu.make_async_copy(w_ref, wrows(c, own, 0, kf), lsem.at[0])
    cw.start()
    cr = pltpu.make_async_copy(r_ref.at[pl.ds(own_rows, blk)], z_ref.at[pl.ds(own_rows, blk)], lsem.at[1])
    cr.start()
    cols_own = pl.ds(own * kf, kf)
    cx = [pltpu.make_async_copy(x_ref.at[c, i, :, pl.ds(n * q, q)], xg.at[n, :, :, cols_own], lsem.at[2 + n])
          for n in range(side)]
    for copy in cx:
        copy.start()

    _barrier((partner, in_p, in_m, red_p, red_m, ot_p, ot_m, from_p, from_m))
    cw.wait()

    for h in (0, 1):
        for up in (1, 0):
            src = wrows(c, own, (h if up else 1 - h) * hk, hk)
            sem = wrel.at[1 - up, c] if h == 0 else wsem
            for cc, slot, dev in ((c, own, in_p if up else in_m), (o, oth, ot_p if up else ot_m)):
                _send(src, wrows(cc, slot, (h if up else 1 - h) * hk, hk), wssem, sem, dev)
    _send(wrows(c, own, 0, kf), wrows(o, oth, 0, kf), wssem, wsem, partner)

    def send_x(n):
        rows = pl.ds(n * q, q)
        for cc, a, up, down in ((c, i, in_p, in_m), (o, j, ot_p, ot_m)):
            cols = pl.ds((a * CORES + c) * kf, kf)
            far = at(a, 2)
            _send(x_ref.at[cc, far, pl.ds(0, hs), rows], xr.at[n, 0, c], xssem, xrel.at[n, 0, c], up)
            _send(x_ref.at[cc, far, pl.ds(hs, hs), rows], xr.at[n, 1, c], xssem, xrel.at[n, 1, c], down)
            _send(x_ref.at[cc, at(a, 1), :, rows], xg.at[n, :, :, cols], xssem, xsem.at[n], up)
            _send(x_ref.at[cc, at(a, -1), :, rows], xg.at[n, :, :, cols], xssem, xsem.at[n], down)
        _send(x_ref.at[o, j, :, rows], xg.at[n, :, :, pl.ds(oth * kf, kf)], xssem, xsem.at[n], partner)

    def pass_x(n):
        for e in range(CORES):
            _wait_recv(xr.at[n, 0, e], xrel.at[n, 0, e], partner)
            _send(xr.at[n, 0, e], xg.at[n, pl.ds(0, hs), :, pl.ds((im * CORES + e) * kf, kf)],
                  xrssem, xsem.at[n], in_p)
            _wait_recv(xr.at[n, 1, e], xrel.at[n, 1, e], partner)
            _send(xr.at[n, 1, e], xg.at[n, pl.ds(hs, hs), :, pl.ds((ip * CORES + e) * kf, kf)],
                  xrssem, xsem.at[n], in_m)

    for e in range(CORES):
        for d, src, dev, first in ((0, im, in_p, 0), (1, ip, in_m, hk)):
            piece = wrows(c, src * CORES + e, first, hk)
            _wait_recv(piece, wrel.at[d, e], partner)
            _send(piece, piece, wssem, wsem, dev)
    send_x(0)
    send_x(1)

    tile = next(t for t in (512, 256, 128) if width % t == 0)
    step = next(t for t in (32, 16, 8) if hq % t == 0)
    depth = side * CORES * kf

    def matmul(n):
        cx[n].wait()
        _wait_recv(xg.at[n, :, :, pl.ds(0, depth - kf)], xsem.at[n], partner)
        w_rows = pl.ds(pl.multiple_of(lent, blk), depth)

        @pl.loop(0, width // tile)
        def _(t):
            cols = pl.ds(pl.multiple_of(t * tile, tile), tile)
            acc[n % 2, :, cols] = jnp.dot(
                xg[n].reshape(side * q, depth), z_ref[w_rows, cols], preferred_element_type=f32)

    def part(n, block, first):
        return acc.at[n % 2, pl.ds(pl.multiple_of(block * q, q) + first, hq)]

    def send_part(n, k, block, first, add, dst, sem, dev):
        src, at_ = part(n, block, first), lent + where[k] + n * q + first

        @pl.loop(0, hq // step)
        def _(t):
            off = pl.multiple_of(t * step, step)
            v = src[pl.ds(off, step), :]
            if add is not None:
                row = lent + where[add] + n * q
                v = v + z_ref[pl.ds(pl.multiple_of(row + off, step), step), :].astype(f32)
            z_ref[pl.ds(pl.multiple_of(at_ + off, step), step), :] = v.astype(z_ref.dtype)

        to = 0 if dst in ("ra", "rb") else first
        _send(z_ref.at[pl.ds(at_, hq)], z_ref.at[buf(dst, n, to, hq)], rssem, sem, dev)

    def first_hop(n):
        send_part(n, "s2", at(j, 2), 0, None, "ra", rsem.at[n, 0], red_p)
        send_part(n, "s2", at(j, 2), hq, None, "rb", rsem.at[n, 1], red_m)
        send_part(n, "sp", jp, hq, None, "fm", rsem.at[n, 2], red_p)
        send_part(n, "sm", jm, 0, None, "fp", rsem.at[n, 3], red_m)

    def keep(n):
        src, dst = acc.at[n % 2, pl.ds(pl.multiple_of(j * q, q), q)], held.at[n % 3]

        @pl.loop(0, q // 8)
        def _(t):
            rows = pl.ds(pl.multiple_of(t * 8, 8), 8)
            dst[rows, :] = src[rows, :]

    def second_hop(n):
        _wait_recv(z_ref.at[buf("ra", n, 0, hq)], rsem.at[n, 0], partner)
        send_part(n, "sp", jp, 0, "ra", "fm", rsem.at[n, 2], red_p)
        _wait_recv(z_ref.at[buf("rb", n, 0, hq)], rsem.at[n, 1], partner)
        send_part(n, "sm", jm, hq, "rb", "fp", rsem.at[n, 3], red_m)

    near = {(0, 1): in_p, (0, -1): in_m, (1, 1): red_p, (1, -1): red_m}

    def piece_of(k, n):
        slot = at(i, k[0]) * side + at(j, k[1])
        return z_ref.at[pl.ds(mine + slot * blk + n * q, q)], slot * side + n

    def both(axis):
        return (axis, 1), (axis, -1)

    def norm(n):
        if n == 0:
            cr.wait()
        _wait_recv(z_ref.at[buf("fm", n, 0, q)], rsem.at[n, 2], partner)
        _wait_recv(z_ref.at[buf("fp", n, 0, q)], rsem.at[n, 3], partner)
        src = held.at[n % 3]

        @pl.loop(0, q // step)
        def _(t):
            off = pl.multiple_of(t * step, step)

            def rows(first):
                return pl.ds(pl.multiple_of(first + n * q + off, step), step)

            y = src[pl.ds(off, step), :] + (
                z_ref[rows(lent + where["fm"]), :].astype(f32) + z_ref[rows(lent + where["fp"]), :].astype(f32))
            a = z_ref[rows(own_rows), :].astype(f32) + y.astype(z_ref.dtype).astype(f32)
            ms = jnp.mean(a * a, axis=-1, keepdims=True)
            z_ref[rows(own_rows), :] = (
                a * lax.rsqrt(ms + EPS) * g_ref[...].astype(f32).reshape(1, width)).astype(z_ref.dtype)

        piece, slot = piece_of((0, 0), n)
        for way in both(n % 2) + both(1 - n % 2):
            _send(piece, piece, gssem, gsem.at[slot], near[way])

    pass_x(0)
    send_x(2)
    pass_x(1)
    send_x(3)
    _wait_recv(z_ref.at[pl.ds(lent, (2 * side * CORES - 6) * hk)], wsem, partner)
    for n in range(side):
        matmul(n)
        first_hop(n)
        keep(n)
        if n + 2 < side:
            pass_x(n + 2)
        if n > 0:
            second_hop(n - 1)
        if n > 1:
            norm(n - 2)
    second_hop(side - 1)
    norm(side - 2)
    norm(side - 1)

    kept = [((0, 0), n) for n in range(side)]

    def take(k, n, ways):
        piece, slot = piece_of(k, n)
        _wait_recv(piece, gsem.at[slot], partner)
        for way in ways:
            _send(piece, piece, gssem, gsem.at[slot], near[way])
        if kept is None:
            _send(piece, piece, gssem, csem, partner)
        else:
            kept.append((k, n))

    def vec(n, d, e=0):
        return (d, e) if n % 2 == 0 else (e, d)

    def onward(n, axis, d):
        return ((axis, -d),) if (n < 2) == (d == -1) else ()

    def second(d1):
        for n in range(side):
            for d in (-1, 1):
                take(vec(n, d1, d), n, onward(n, 1 - n % 2, d))

    def far(d1):
        for n in range(side):
            take(vec(n, d1, 2), n, ())

    for n in range(side):
        for d in (-1, 1):
            take(vec(n, d), n, onward(n, n % 2, d) + both(1 - n % 2))

    _wait_send(z_ref.at[pl.ds(lent, 7 * kf)], wssem, partner)
    _wait_send(z_ref.at[pl.ds(lent, 3 * blk)], rssem, partner)
    pl.semaphore_signal(credit, inc=1, device_id={"tp": partner}, device_id_type=MESH)
    second(0)
    for n in range(side):
        take(vec(n, 2), n, both(1 - n % 2))
    pl.semaphore_wait(credit, 1)
    for k, n in kept:
        piece, _ = piece_of(k, n)
        _send(piece, piece, gssem, csem, partner)
    kept = None
    second(-1)
    second(1)
    far(0)
    second(2)
    far(-1)
    far(1)
    far(2)
    count = side * side * side
    _wait_recv(z_ref.at[pl.ds(0, count * q)], csem, partner)
    _wait_send(z_ref.at[pl.ds(0, (2 * count - side) * q)], gssem, partner)
    _wait_send(xg.at[:, :, :, pl.ds(0, depth - kf)], xssem, partner)
    _wait_send(xg.at[:, :, :, pl.ds(0, 2 * kf)], xrssem, partner)


def _store_kernel(z_ref, o_ref, sem):
    n = 16
    rows = z_ref.shape[0] // n
    cs = [pltpu.make_async_copy(z_ref.at[pl.ds(k * rows, rows)], o_ref.at[pl.ds(k * rows, rows)], sem.at[k]) for k in range(n)]
    for c in cs:
        c.start()
    for c in cs:
        c.wait()


def solution(mesh):
    tp = mesh.shape["tp"]
    side = math.isqrt(tp // CORES)

    def local(x, w, r, g):
        total, kf = x.shape
        width = w.shape[1]
        blk = total // tp
        bf = jnp.bfloat16
        dma = pltpu.SemaphoreType.DMA
        any_ = pl.BlockSpec(memory_space=pl.ANY)
        vmem = pl.BlockSpec(memory_space=pltpu.VMEM)
        z = pl.pallas_call(
            functools.partial(_fused_kernel, side),
            out_shape=pltpu.VMEM(r.shape, bf),
            in_specs=[any_, any_, any_, vmem],
            out_specs=vmem,
            scratch_shapes=[
                pltpu.VMEM((side, side, blk // side, side * CORES * kf), bf),
                pltpu.VMEM((side, 2, CORES, side // 2, blk // side, kf), bf),
                pltpu.VMEM((2, blk, width), jnp.float32),
                pltpu.VMEM((3, blk // side, width), jnp.float32),
                dma((2 + side,)), dma((2, CORES)), dma, dma,
                dma((side, 2, CORES)), dma((side,)), dma, dma,
                dma((side, 4)), dma, pltpu.SemaphoreType.REGULAR,
                dma((side * side * side,)), dma, dma,
            ],
            compiler_params=pltpu.CompilerParams(
                collective_id=0, has_side_effects=True, vmem_limit_bytes=63 * 2**18),
            name="fused",
        )(x.reshape(CORES, side, side, blk, kf), w, r, g)
        return pl.pallas_call(
            _store_kernel,
            out_shape=pltpu.HBM(r.shape, bf),
            in_specs=[vmem],
            out_specs=pl.BlockSpec(memory_space=pltpu.HBM),
            scratch_shapes=[dma((16,))],
            compiler_params=pltpu.CompilerParams(vmem_limit_bytes=2**20),
            name="store",
        )(z)

    return jax.shard_map(
        local,
        mesh=mesh,
        in_specs=(P("data", "tp"), P("tp", None), P("data", None), P(None)),
        out_specs=P("data", None),
        check_vma=False,
    )
```

time: 444 us -> 256 us (0.58)
  waiting for transfers between devices: 366 us -> 0 us
  Pallas kernels: 0 us -> 256 us
  local copies, waits for them, and re-layouts: 36 us -> 0 us
  matrix products: 22.8 us -> 0 us
  between operations: 13.5 us -> 0.01 us
  other arithmetic: 5.87 us -> 0 us
    pallas_call x0 -> x2, Pallas kernels: none -> 256 us  [the longest x1 240 us: local(): pl.pallas_call(functools.partial(_fused_kernel, side), out_shape=pltpu.VM...]
    reduce_scatter x1 -> x0, waiting for transfers between devices: 213 us -> none  [local(): y = lax.psum_scatter(p, 'tp', scatter_dimension=0, tiled=True)]
    all_gather x1 -> x0, waiting for transfers between devices: 153 us -> none  [local(): return lax.all_gather(zl, 'tp', axis=0, tiled=True)]
    unnamed x9 -> x0, local copies, waits for them, and re-layouts: 36 us -> none
    dot_general x1 -> x0, matrix products: 22.8 us -> none  [local(): p = jnp.dot(x, w, preferred_element_type=jnp.float32).astype(jnp.bfloat16)]
  transfers between devices with their start and end apart: 2 -> 0, of which waited for: 2 -> 0; matrix products, arithmetic and copies ran while one was open for 0% -> 0% of each run, Pallas kernels for 0% -> 0%
where the time goes in v2:
time: 256 us
  Pallas kernels  256 us (100%)
    pallas_call x1, Pallas kernels, local(): pl.pallas_call(functools.partial(_fused_kernel, side), out_shape=pltpu.VM...  240 us
    pallas_call x1, Pallas kernels, local(): pl.pallas_call(_store_kernel, out_shape=pltpu.HBM(r.shape, bf), in_specs=...  16.2 us

profile of v2, /device:TPU:97, one launch (start us, length us, event | category | flops | bytes accessed | tf_op | source)
XLA Modules:
  0.0 255.8 jit_solution(416089513513084002)
XLA Ops:
  0.0 239.6 %fused.1.z_ref = bf16[8192,3072]{1,0:T(8,128)(2,1)S(1)} custom-call(bf16[2,4,4,256,256]{4,3,2,1,0:T(8,128)(2,1)} %bitcast.1, bf16[256,3072]{1,0:T(8,128)(2,1)} %w_ref.1, bf16[8192,3072]{1,0:T(8,128)(2,1)} %r_ref.1, bf16[3072]{0:T(1024)(128)(2,1)} %g_ref.1), custom_call_target="tpu_custom_call" | custom-call | tf_op jit(solution)/shard_map/fused/pallas_call | solution.py:327
  239.6 16.2 %store.1 = bf16[8192,3072]{1,0:T(8,128)(2,1)} custom-call(bf16[8192,3072]{1,0:T(8,128)(2,1)S(1)} %fused.1.z_ref), custom_call_target="tpu_custom_call" | custom-call | tf_op jit(solution)/shard_map/store/pallas_call | solution.py:346

commit v3 on v2

v3 whole, which is shorter than its diff:
```python
import functools
import math

import jax
import jax.numpy as jnp
from jax import lax
from jax.experimental import pallas as pl
from jax.experimental.pallas import tpu as pltpu
from jax.sharding import PartitionSpec as P

EPS = 1e-6
CORES = 2
MESH = pl.DeviceIdType.MESH


def _place(side):
    me = lax.axis_index("tp")
    c = lax.rem(me, CORES)
    chip = lax.div(me, CORES)
    xx, yy = lax.rem(chip, side), lax.div(chip, side)
    return me, c, xx + (yy - xx) * c, yy + (xx - yy) * c


def _dev(side, c, i, j):
    return CORES * (i * (1 + (side - 1) * c) + j * (side - (side - 1) * c)) + c


def _send(src, dst, ssem, rsem, dev):
    pltpu.make_async_remote_copy(
        src_ref=src, dst_ref=dst, send_sem=ssem, recv_sem=rsem,
        device_id={"tp": dev}, device_id_type=MESH,
    ).start()


def _wait_recv(ref, sem, dev):
    pltpu.make_async_remote_copy(
        src_ref=ref, dst_ref=ref, send_sem=sem, recv_sem=sem,
        device_id={"tp": dev}, device_id_type=MESH,
    ).wait_recv()


def _wait_send(ref, sem, dev):
    pltpu.make_async_remote_copy(
        src_ref=ref, dst_ref=ref, send_sem=sem, recv_sem=sem,
        device_id={"tp": dev}, device_id_type=MESH,
    ).wait_send()


def _barrier(devs):
    bar = pltpu.get_barrier_semaphore()
    for d in devs:
        pl.semaphore_signal(bar, inc=1, device_id={"tp": d}, device_id_type=MESH)
    pl.semaphore_wait(bar, len(devs))


def _fused_kernel(
    side, x_ref, w_ref, r_ref, g_ref, z_ref,
    xo, acc, held, gain, sums, stat_out, stat_in,
    lsem, wrel, wsem, wssem, xrel, xsem, xssem, xrssem, rsem, rssem, tsem, tssem, credit, gsem, csem, gssem,
):
    me, c, i, j = _place(side)
    o = 1 - c
    halves, groups, q, hw = z_ref.shape
    width = halves * hw
    kf = x_ref.shape[-1]
    hq = q // 2
    kg = kf // q
    per_core = groups // CORES
    f32 = jnp.float32
    bf = z_ref.dtype

    def at(v, d):
        return lax.rem(v + d + side, side)

    def nh(a):
        return lax.div(a, side // 2)

    def mh(a):
        return lax.rem(lax.div(a + 1, 2), 2)

    def near_n(a):
        return a + 1 - 2 * lax.rem(a, 2)

    def near_m(a):
        return at(a, 2 * lax.rem(a, 2) - 1)

    jp, jm = at(j, 1), at(j, -1)
    partner = _dev(side, o, j, i)
    in_p, in_m = _dev(side, c, at(i, 1), j), _dev(side, c, at(i, -1), j)
    red_p, red_m = _dev(side, c, i, jp), _dev(side, c, i, jm)
    lines = []
    for cc, a, b in ((c, i, j), (o, j, i)):
        lines.append((cc, a, _dev(side, cc, near_n(a), b), _dev(side, cc, near_m(a), b)))
    from_p, from_m = _dev(side, o, j, at(i, 1)), _dev(side, o, j, at(i, -1))
    to_n, to_m = lines[0][2:]

    def cols_of(h):
        return pl.ds(pl.multiple_of(h * hw, hw), hw)

    def lent(cc, half, first, size):
        return half, pl.ds((1 - cc) * per_core + first, size)

    def w_at(cc, role, core):
        h, g = lent(cc, 0, (role * CORES + core) * kg, kg)
        return z_ref.at[h, g]

    x_first = side * CORES * kg

    def x_at(cc, n, role, core):
        if role == 3:
            return xo.at[n, :, :, pl.ds(core * kf, kf)]
        h, g = lent(cc, 0, x_first + n * side, side)
        return z_ref.at[h, g, :, pl.ds((role * CORES + core) * kf, kf)]

    names = ("s2", "sp", "sm", "fm", "fp", "ra", "rb")
    base = o * per_core

    def buf(k, n):
        return base + names.index(k) * side + n

    def own_group(ii, jj):
        return nh(ii), ((c * 2 + mh(ii)) * side + jj) * side

    my_half, my_group = own_group(i, j)

    cw = pltpu.make_async_copy(w_ref.at[:, :, cols_of(nh(i))], w_at(c, 0, c), lsem.at[0])
    cw.start()
    cr = pltpu.make_async_copy(
        r_ref.at[pl.ds(my_group, side), :, cols_of(nh(i))], z_ref.at[my_half, pl.ds(my_group, side)], lsem.at[1])
    cr.start()
    cx = [pltpu.make_async_copy(x_ref.at[c, mh(i), :, pl.ds(n * q, q)], x_at(c, n, 0, c), lsem.at[2 + n])
          for n in range(side)]
    for copy in cx:
        copy.start()

    _barrier((partner, in_p, in_m, red_p, red_m, lines[1][2], lines[1][3], from_p, from_m))

    for cc, a, dev_n, dev_m in lines:
        _send(w_ref.at[:, :, cols_of(1 - nh(a))], w_at(cc, 2, c), wssem, wrel.at[c], dev_m)
    for cc, a, dev_n, dev_m in lines:
        _send(w_ref.at[:, :, cols_of(nh(a))], w_at(cc, 1, c), wssem, wsem, dev_n)
    _send(w_ref.at[:, :, cols_of(nh(j))], w_at(o, 0, c), wssem, wsem, partner)

    def send_x(n):
        rows = pl.ds(n * q, q)
        for cc, a, dev_n, dev_m in lines:
            _send(x_ref.at[cc, mh(a), :, rows], x_at(cc, n, 2, c), xssem, xsem.at[n], dev_m)
        _send(x_ref.at[o, mh(j), :, rows], x_at(o, n, 0, c), xssem, xsem.at[n], partner)

    def relay_x(n, line):
        cc, a, dev_n, dev_m = line
        _send(x_ref.at[cc, 1 - mh(a), :, pl.ds(n * q, q)], x_at(cc, n, 1, c), xssem, xrel.at[n, c], dev_n)

    def pass_x(n):
        for e in range(CORES):
            piece = x_at(c, n, 1, e)
            _wait_recv(piece, xrel.at[n, e], partner)
            _send(piece, x_at(c, n, 3, e), xrssem, xsem.at[n], to_m)

    for n in range(side):
        send_x(n)

    gain[...] = jnp.where(
        my_half == 0, g_ref[...].astype(f32).reshape(1, width)[:, :hw], g_ref[...].astype(f32).reshape(1, width)[:, hw:])

    for line in lines:
        relay_x(0, line)
    for e in range(CORES):
        piece = w_at(c, 2, e)
        _wait_recv(piece, wrel.at[e], partner)
        _send(piece, w_at(c, 3, e), wssem, wsem, to_n)
    for line in lines:
        relay_x(1, line)
    pass_x(0)
    for line in lines:
        relay_x(2, line)
    pass_x(1)
    for line in lines:
        relay_x(3, line)
    _wait_recv(z_ref.at[0, pl.ds(base, 5 * kg)], wsem, partner)
    cw.wait()

    tile = next(t for t in (512, 256, 128) if hw % t == 0)
    step = next(t for t in (32, 16, 8) if hq % t == 0)
    roles = 3 * CORES

    def x_wait_ref(first, size, pieces):
        return z_ref.at[0, pl.ds(base + x_first + first, size), :, pl.ds(0, pieces * kf)]

    def matmul(n):
        cx[n].wait()
        _wait_recv(x_wait_ref(n * side, side, 5), xsem.at[n], partner)

        @pl.loop(0, hw // tile)
        def _(t):
            cols = pl.ds(pl.multiple_of(t * tile, tile), tile)
            near = jnp.dot(
                z_ref[0, pl.ds(base + x_first + n * side, side), :, pl.ds(0, roles * kf)].reshape(side * q, roles * kf),
                z_ref[0, pl.ds(base, roles * kg), :, cols].reshape(roles * kf, tile), preferred_element_type=f32)
            acc[n % 2, :, cols] = near + jnp.dot(
                xo[n].reshape(side * q, CORES * kf),
                z_ref[0, pl.ds(base + roles * kg, CORES * kg), :, cols].reshape(CORES * kf, tile),
                preferred_element_type=f32)

    def part(n, block, first, size):
        return acc.at[n % 2, pl.ds(pl.multiple_of(block * q, q) + first, size)]

    def send_part(n, k, block, first, add, dst, sem, dev):
        src = part(n, block, first, hq)

        @pl.loop(0, hq // step)
        def _(t):
            off = pl.multiple_of(t * step, step)
            v = src[pl.ds(off, step), :]
            if add is not None:
                v = v + z_ref[1, buf(add, n), pl.ds(off, step), :].astype(f32)
            z_ref[1, buf(k, n), pl.ds(first + off, step), :] = v.astype(bf)

        to = 0 if dst in ("ra", "rb") else first
        _send(z_ref.at[1, buf(k, n), pl.ds(first, hq)], z_ref.at[1, buf(dst, n), pl.ds(to, hq)], rssem, sem, dev)

    def first_hop(n):
        send_part(n, "s2", at(j, 2), 0, None, "ra", rsem.at[n, 0], red_p)
        send_part(n, "s2", at(j, 2), hq, None, "rb", rsem.at[n, 1], red_m)
        send_part(n, "sp", jp, hq, None, "fm", rsem.at[n, 2], red_p)
        send_part(n, "sm", jm, 0, None, "fp", rsem.at[n, 3], red_m)
        src = part(n, j, 0, q)

        @pl.loop(0, q // step)
        def _(t):
            rows = pl.ds(pl.multiple_of(t * step, step), step)
            held[n, rows, :] = src[rows, :]

    def second_hop(n):
        _wait_recv(z_ref.at[1, buf("ra", n), pl.ds(0, hq)], rsem.at[n, 0], partner)
        send_part(n, "sp", jp, 0, "ra", "fm", rsem.at[n, 2], red_p)
        _wait_recv(z_ref.at[1, buf("rb", n), pl.ds(0, hq)], rsem.at[n, 1], partner)
        send_part(n, "sm", jm, hq, "rb", "fp", rsem.at[n, 3], red_m)

    def add_up(n):
        if n == 0:
            cr.wait()
        _wait_recv(z_ref.at[1, buf("fm", n)], rsem.at[n, 2], partner)
        _wait_recv(z_ref.at[1, buf("fp", n)], rsem.at[n, 3], partner)

        @pl.loop(0, q // step)
        def _(t):
            rows = pl.ds(pl.multiple_of(t * step, step), step)
            y = held[n, rows, :] + (
                z_ref[1, buf("fm", n), rows, :].astype(f32) + z_ref[1, buf("fp", n), rows, :].astype(f32))
            v = z_ref[my_half, my_group + n, rows, :].astype(f32) + y.astype(bf).astype(f32)
            held[n, rows, :] = v
            sums[n, rows, :] = jnp.broadcast_to(jnp.sum(v * v, axis=-1, keepdims=True), (step, sums.shape[-1]))

        stat_out[n] = sums[n].T[:8]
        _send(stat_out.at[n], stat_in.at[n], tssem, tsem.at[n], to_m)

    near = {(0, 1): in_p, (0, -1): in_m, (1, 1): red_p, (1, -1): red_m}

    def piece_of(k, n):
        ii, jj = at(i, k[0]), at(j, k[1])
        h, g = own_group(ii, jj)
        return z_ref.at[h, g + n], (ii * side + jj) * side + n

    def both(axis):
        return (axis, 1), (axis, -1)

    def norm(n):
        _wait_recv(stat_in.at[n], tsem.at[n], partner)
        theirs = jnp.broadcast_to(stat_in[n][:1], (sums.shape[-1], q)).T
        sums[n] = lax.rsqrt((sums[n] + theirs) * (1.0 / width) + EPS)

        @pl.loop(0, q // step)
        def _(t):
            rows = pl.ds(pl.multiple_of(t * step, step), step)
            z_ref[my_half, my_group + n, rows, :] = (held[n, rows, :] * sums[n, rows, :1] * gain[...]).astype(bf)

        piece, slot = piece_of((0, 0), n)
        for way in both(n % 2) + both(1 - n % 2):
            _send(piece, piece, gssem, gsem.at[slot], near[way])

    for n in range(side):
        matmul(n)
        first_hop(n)
        if n + 2 < side:
            pass_x(n + 2)
        if n > 0:
            second_hop(n - 1)
        if n > 2:
            norm(n - 3)
        if n > 1:
            add_up(n - 2)
    second_hop(side - 1)
    norm(side - 3)
    add_up(side - 2)
    add_up(side - 1)
    norm(side - 2)
    norm(side - 1)

    kept = [((0, 0), n) for n in range(side)]

    def take(k, n, ways):
        piece, slot = piece_of(k, n)
        _wait_recv(piece, gsem.at[slot], partner)
        for way in ways:
            _send(piece, piece, gssem, gsem.at[slot], near[way])
        if kept is None:
            _send(piece, piece, gssem, csem, partner)
        else:
            kept.append((k, n))

    def vec(n, d, e=0):
        return (d, e) if n % 2 == 0 else (e, d)

    def onward(n, axis, d):
        return ((axis, -d),) if (n < 2) == (d == -1) else ()

    def second(d1):
        for n in range(side):
            for d in (-1, 1):
                take(vec(n, d1, d), n, onward(n, 1 - n % 2, d))

    def far(d1):
        for n in range(side):
            take(vec(n, d1, 2), n, ())

    for n in range(side):
        for d in (-1, 1):
            take(vec(n, d), n, onward(n, n % 2, d) + both(1 - n % 2))

    _wait_send(z_ref.at[0, pl.ds(base, 7 * kg)], wssem, partner)
    _wait_send(x_wait_ref(0, side * side, 2), xrssem, partner)
    _wait_send(z_ref.at[1, pl.ds(base, 3 * side)], rssem, partner)
    pl.semaphore_signal(credit, inc=1, device_id={"tp": partner}, device_id_type=MESH)
    second(0)
    for n in range(side):
        take(vec(n, 2), n, both(1 - n % 2))
    pl.semaphore_wait(credit, 1)
    for k, n in kept:
        piece, _ = piece_of(k, n)
        _send(piece, piece, gssem, csem, partner)
    kept = None
    second(-1)
    second(1)
    far(0)
    second(2)
    far(-1)
    far(1)
    far(2)
    count = side * side * side
    _wait_recv(z_ref.at[0, pl.ds(0, count)], csem, partner)
    _wait_send(z_ref.at[:, pl.ds(0, count - side // 2)], gssem, partner)
    _wait_send(x_wait_ref(0, side * side, 5), xssem, partner)
    _wait_send(stat_out, tssem, partner)


def _store_kernel(z_ref, o_ref, sem):
    halves, groups, _, hw = z_ref.shape
    n = groups // 8
    copies = [
        pltpu.make_async_copy(
            z_ref.at[h, pl.ds(k * n, n)], o_ref.at[pl.ds(k * n, n), :, pl.ds(h * hw, hw)], sem.at[h, k])
        for k in range(8) for h in range(halves)
    ]
    for copy in copies:
        copy.start()
    for copy in copies:
        copy.wait()


def solution(mesh):
    tp = mesh.shape["tp"]
    side = math.isqrt(tp // CORES)

    def local(x, w, r, g):
        total, kf = x.shape
        width = w.shape[1]
        blk = total // tp
        bf = jnp.bfloat16
        dma = pltpu.SemaphoreType.DMA
        any_ = pl.BlockSpec(memory_space=pl.ANY)
        vmem = pl.BlockSpec(memory_space=pltpu.VMEM)
        q = blk // 2
        hw = width // 2
        groups = total // q
        z = pl.pallas_call(
            functools.partial(_fused_kernel, side),
            out_shape=pltpu.VMEM((2, groups, q, hw), bf),
            in_specs=[any_, any_, any_, vmem],
            out_specs=vmem,
            scratch_shapes=[
                pltpu.VMEM((side, side, q, CORES * kf), bf),
                pltpu.VMEM((2, side * q, hw), jnp.float32),
                pltpu.VMEM((side, q, hw), jnp.float32),
                pltpu.VMEM((1, hw), jnp.float32),
                pltpu.VMEM((side, q, 128), jnp.float32),
                pltpu.VMEM((side, 8, q), jnp.float32),
                pltpu.VMEM((side, 8, q), jnp.float32),
                dma((2 + side,)), dma((CORES,)), dma, dma,
                dma((side, CORES)), dma((side,)), dma, dma,
                dma((side, 4)), dma, dma((side,)), dma, pltpu.SemaphoreType.REGULAR,
                dma((side * side * side,)), dma, dma,
            ],
            compiler_params=pltpu.CompilerParams(
                collective_id=0, has_side_effects=True, vmem_limit_bytes=63 * 2**18),
            name="fused",
        )(x.reshape(CORES, 2, side, side * q, kf), w.reshape(kf // q, q, width), r.reshape(groups, q, width), g)
        out = pl.pallas_call(
            _store_kernel,
            out_shape=pltpu.HBM((groups, q, width), bf),
            in_specs=[vmem],
            out_specs=pl.BlockSpec(memory_space=pltpu.HBM),
            scratch_shapes=[dma((2, 8))],
            compiler_params=pltpu.CompilerParams(vmem_limit_bytes=2**20),
            name="store",
        )(z)
        return out.reshape(r.shape)

    return jax.shard_map(
        local,
        mesh=mesh,
        in_specs=(P("data", "tp"), P("tp", None), P("data", None), P(None)),
        out_specs=P("data", None),
        check_vma=False,
    )
```

time: 256 us -> 249 us (0.973)
  Pallas kernels: 256 us -> 249 us
    pallas_call x1, Pallas kernels: 240 us -> 233 us  [local(): pl.pallas_call(functools.partial(_fused_kernel, side), out_shape=pltpu.VM...]
where the time goes in v3:
time: 249 us
  Pallas kernels  249 us (100%)
    pallas_call x1, Pallas kernels, local(): pl.pallas_call(functools.partial(_fused_kernel, side), out_shape=pltpu.VM...  233 us
    pallas_call x1, Pallas kernels, local(): pl.pallas_call(_store_kernel, out_shape=pltpu.HBM((groups, q, width), bf)...  16.2 us

profile of v3, /device:TPU:97, one launch (start us, length us, event | category | flops | bytes accessed | tf_op | source)
XLA Modules:
  0.0 249.1 jit_solution(18021459754501264556)
XLA Ops:
  0.0 232.9 %fused.1.z_ref = bf16[2,64,128,1536]{3,2,1,0:T(8,128)(2,1)S(1)} custom-call(bf16[2,2,4,512,256]{4,3,2,1,0:T(8,128)(2,1)} %bitcast.5, bf16[2,128,3072]{2,1,0:T(8,128)(2,1)} %bitcast.6, bf16[64,128,3072]{2,1,0:T(8,128)(2,1)} %bitcast.4, bf16[3072]{0:T(1024)(128)(2,1)} %g_ref.1), custom_call_target="tpu_custom_call" | custom-call | tf_op jit(solution)/shard_map/fused/pallas_call | solution.py:386
  233.0 16.2 %store.1 = bf16[64,128,3072]{2,1,0:T(8,128)(2,1)} custom-call(bf16[2,64,128,1536]{3,2,1,0:T(8,128)(2,1)S(1)} %fused.1.z_ref), custom_call_target="tpu_custom_call" | custom-call | tf_op jit(solution)/shard_map/store/pallas_call | solution.py:408

commit v4 on v3

--- a/solution.py
+++ b/solution.py
@@ -10,6 +10,7 @@
 
 EPS = 1e-6
 CORES = 2
+PARTS = 4
 MESH = pl.DeviceIdType.MESH
 
 
@@ -55,8 +56,8 @@
 
 def _fused_kernel(
     side, x_ref, w_ref, r_ref, g_ref, z_ref,
-    xo, acc, held, gain, sums, stat_out, stat_in,
-    lsem, wrel, wsem, wssem, xrel, xsem, xssem, xrssem, rsem, rssem, tsem, tssem, credit, gsem, csem, gssem,
+    xo, acc, held, gv, gain, sums, stat_out, stat_in,
+    lsem, wrel, wsem, wssem, xrel, xsem, xssem, xrssem, rsem, rssem, tsem, tssem, credit, gsem, lsts, csem, gssem,
 ):
     me, c, i, j = _place(side)
     o = 1 - c
@@ -128,6 +129,8 @@
     cr = pltpu.make_async_copy(
         r_ref.at[pl.ds(my_group, side), :, cols_of(nh(i))], z_ref.at[my_half, pl.ds(my_group, side)], lsem.at[1])
     cr.start()
+    cg = pltpu.make_async_copy(g_ref, gv, lsem.at[2 + side])
+    cg.start()
     cx = [pltpu.make_async_copy(x_ref.at[c, mh(i), :, pl.ds(n * q, q)], x_at(c, n, 0, c), lsem.at[2 + n])
           for n in range(side)]
     for copy in cx:
@@ -157,18 +160,21 @@
             _wait_recv(piece, xrel.at[n, e], partner)
             _send(piece, x_at(c, n, 3, e), xrssem, xsem.at[n], to_m)
 
-    for n in range(side):
-        send_x(n)
-
+    cg.wait()
     gain[...] = jnp.where(
-        my_half == 0, g_ref[...].astype(f32).reshape(1, width)[:, :hw], g_ref[...].astype(f32).reshape(1, width)[:, hw:])
-
-    for line in lines:
-        relay_x(0, line)
-    for e in range(CORES):
+        my_half == 0, gv[...].astype(f32).reshape(1, width)[:, :hw], gv[...].astype(f32).reshape(1, width)[:, hw:])
+
+    def pass_w(e):
         piece = w_at(c, 2, e)
         _wait_recv(piece, wrel.at[e], partner)
         _send(piece, w_at(c, 3, e), wssem, wsem, to_n)
+
+    for n in range(side):
+        send_x(n)
+    for line in lines:
+        relay_x(0, line)
+    pass_w(0)
+    pass_w(1)
     for line in lines:
         relay_x(1, line)
     pass_x(0)
@@ -177,6 +183,8 @@
     pass_x(1)
     for line in lines:
         relay_x(3, line)
+    pass_x(2)
+    pass_x(3)
     _wait_recv(z_ref.at[0, pl.ds(base, 5 * kg)], wsem, partner)
     cw.wait()
 
@@ -282,8 +290,6 @@
     for n in range(side):
         matmul(n)
         first_hop(n)
-        if n + 2 < side:
-            pass_x(n + 2)
         if n > 0:
             second_hop(n - 1)
         if n > 2:
@@ -299,11 +305,18 @@
 
     kept = [((0, 0), n) for n in range(side)]
 
-    def take(k, n, ways):
+    size = q // PARTS
+
+    def take(k, n, ways, last=False):
         piece, slot = piece_of(k, n)
         _wait_recv(piece, gsem.at[slot], partner)
         for way in ways:
-            _send(piece, piece, gssem, gsem.at[slot], near[way])
+            if last:
+                for m in range(PARTS):
+                    bit = piece.at[pl.ds(m * size, size)]
+                    _send(bit, bit, gssem, lsts.at[n, m], near[way])
+            else:
+                _send(piece, piece, gssem, gsem.at[slot], near[way])
         if kept is None:
             _send(piece, piece, gssem, csem, partner)
         else:
@@ -318,7 +331,7 @@
     def second(d1):
         for n in range(side):
             for d in (-1, 1):
-                take(vec(n, d1, d), n, onward(n, 1 - n % 2, d))
+                take(vec(n, d1, d), n, onward(n, 1 - n % 2, d), d1 == 2)
 
     def far(d1):
         for n in range(side):
@@ -346,7 +359,11 @@
     second(2)
     far(-1)
     far(1)
-    far(2)
+    for m in range(PARTS):
+        for n in range(side):
+            bit = piece_of(vec(n, 2, 2), n)[0].at[pl.ds(m * size, size)]
+            _wait_recv(bit, lsts.at[n, m], partner)
+            _send(bit, bit, gssem, csem, partner)
     count = side * side * side
     _wait_recv(z_ref.at[0, pl.ds(0, count)], csem, partner)
     _wait_send(z_ref.at[:, pl.ds(0, count - side // 2)], gssem, partner)
@@ -386,20 +403,21 @@
         z = pl.pallas_call(
             functools.partial(_fused_kernel, side),
             out_shape=pltpu.VMEM((2, groups, q, hw), bf),
-            in_specs=[any_, any_, any_, vmem],
+            in_specs=[any_, any_, any_, any_],
             out_specs=vmem,
             scratch_shapes=[
                 pltpu.VMEM((side, side, q, CORES * kf), bf),
                 pltpu.VMEM((2, side * q, hw), jnp.float32),
                 pltpu.VMEM((side, q, hw), jnp.float32),
+                pltpu.VMEM((width,), bf),
                 pltpu.VMEM((1, hw), jnp.float32),
                 pltpu.VMEM((side, q, 128), jnp.float32),
                 pltpu.VMEM((side, 8, q), jnp.float32),
                 pltpu.VMEM((side, 8, q), jnp.float32),
-                dma((2 + side,)), dma((CORES,)), dma, dma,
+                dma((3 + side,)), dma((CORES,)), dma, dma,
                 dma((side, CORES)), dma((side,)), dma, dma,
                 dma((side, 4)), dma, dma((side,)), dma, pltpu.SemaphoreType.REGULAR,
-                dma((side * side * side,)), dma, dma,
+                dma((side * side * side,)), dma((side, PARTS)), dma, dma,
             ],
             compiler_params=pltpu.CompilerParams(
                 collective_id=0, has_side_effects=True, vmem_limit_bytes=63 * 2**18),

time: 249 us -> 247 us (level)
  no operation moved by 1% of the time
where the time goes in v4:
time: 247 us
  Pallas kernels  247 us (100%)
    pallas_call x1, Pallas kernels, local(): pl.pallas_call(functools.partial(_fused_kernel, side), out_shape=pltpu.VM...  231 us
    pallas_call x1, Pallas kernels, local(): pl.pallas_call(_store_kernel, out_shape=pltpu.HBM((groups, q, width), bf)...  16.2 us

profile of v4, /device:TPU:97, one launch (start us, length us, event | category | flops | bytes accessed | tf_op | source)
XLA Modules:
  0.0 247.0 jit_solution(17522589630366575672)
XLA Ops:
  0.0 230.8 %fused.1.z_ref = bf16[2,64,128,1536]{3,2,1,0:T(8,128)(2,1)S(1)} custom-call(bf16[2,2,4,512,256]{4,3,2,1,0:T(8,128)(2,1)} %bitcast.5, bf16[2,128,3072]{2,1,0:T(8,128)(2,1)} %bitcast.6, bf16[64,128,3072]{2,1,0:T(8,128)(2,1)} %bitcast.4, bf16[3072]{0:T(1024)(128)(2,1)} %g_ref.1), custom_call_target="tpu_custom_call" | custom-call | tf_op jit(solution)/shard_map/fused/pallas_call | solution.py:403
  230.8 16.2 %store.1 = bf16[64,128,3072]{2,1,0:T(8,128)(2,1)} custom-call(bf16[2,64,128,1536]{3,2,1,0:T(8,128)(2,1)S(1)} %fused.1.z_ref), custom_call_target="tpu_custom_call" | custom-call | tf_op jit(solution)/shard_map/store/pallas_call | solution.py:426

commit v5 on v4

--- a/solution.py
+++ b/solution.py
@@ -10,7 +10,7 @@
 
 EPS = 1e-6
 CORES = 2
-PARTS = 4
+PARTS = 8
 MESH = pl.DeviceIdType.MESH
 
 

time: 247 us -> 247 us (level)
  no operation moved by 1% of the time
where the time goes in v5:
time: 247 us
  Pallas kernels  247 us (100%)
    pallas_call x1, Pallas kernels, local(): pl.pallas_call(functools.partial(_fused_kernel, side), out_shape=pltpu.VM...  231 us
    pallas_call x1, Pallas kernels, local(): pl.pallas_call(_store_kernel, out_shape=pltpu.HBM((groups, q, width), bf)...  16.2 us

profile of v5, /device:TPU:97, one launch (start us, length us, event | category | flops | bytes accessed | tf_op | source)
XLA Modules:
  0.0 246.8 jit_solution(1129699872467528596)
XLA Ops:
  0.0 230.7 %fused.1.z_ref = bf16[2,64,128,1536]{3,2,1,0:T(8,128)(2,1)S(1)} custom-call(bf16[2,2,4,512,256]{4,3,2,1,0:T(8,128)(2,1)} %bitcast.5, bf16[2,128,3072]{2,1,0:T(8,128)(2,1)} %bitcast.6, bf16[64,128,3072]{2,1,0:T(8,128)(2,1)} %bitcast.4, bf16[3072]{0:T(1024)(128)(2,1)} %g_ref.1), custom_call_target="tpu_custom_call" | custom-call | tf_op jit(solution)/shard_map/fused/pallas_call | solution.py:403
  230.7 16.2 %store.1 = bf16[64,128,3072]{2,1,0:T(8,128)(2,1)} custom-call(bf16[2,64,128,1536]{3,2,1,0:T(8,128)(2,1)S(1)} %fused.1.z_ref), custom_call_target="tpu_custom_call" | custom-call | tf_op jit(solution)/shard_map/store/pallas_call | solution.py:426
